TPU v7x, 128 devices: a whole 4x4x4 slice. The times are simulated.
128 devices in a mesh: ga: 32 (over z, y, core), ba: 4 (over x).
Axes of the slice: x: 4, y: 4, z: 4, core: 2. Of those that a mesh axis runs over, the one named last changes fastest.
Arguments:
- coefficients: bfloat16 [40960, 6144], P('ga', 'ba')
- rotation: bfloat16 [6144, 6144], P('ga', 'ba'), may hold values from -0.078125 to 0.078125
Outputs:
- new_coefficients: bfloat16 [40960, 6144], P('ga', 'ba')
- band_rms: float32 [6144], P('ba')
All inputs are finite; a program needn't handle non-finite values.
Results may differ from a plain program's by a relative error of at most 0.0004.
Values may be sent and summed in bfloat16 or wider, within the bound.
No kernel may reach another device: no remote copies, remote signals or barrier semaphores. Data moves between devices by JAX's collectives and lax.ppermute only.
A program may use at most 128 MiB of HBM per device.

v0:
```python
import jax
import jax.numpy as jnp
from jax import lax
from jax.sharding import PartitionSpec as P


def copy_for_each(array, axis):
    copies = jnp.broadcast_to(array, (lax.axis_size(axis), *array.shape))
    return lax.all_to_all(copies, axis, split_axis=0, concat_axis=0, tiled=True)


def joined_along(blocks, dim):
    shape = list(blocks.shape[1:])
    shape[dim] *= blocks.shape[0]
    return jnp.moveaxis(blocks, 0, dim).reshape(shape)


def gather_directly(array, axis, dim):
    blocks = copy_for_each(array, axis)
    return joined_along(blocks, dim)


def over_copies(array, axis):
    everything = copy_for_each(array, axis)
    return jnp.sum(everything, axis=0)


def body(coefficients, rotation):
    column_block = lax.all_gather(rotation, "ga", axis=0, tiled=True)
    rotated = jnp.dot(
        gather_directly(coefficients, "ba", 1), column_block, preferred_element_type=jnp.float32
    )
    squares = over_copies(jnp.sum(rotated * rotated, axis=0), "ga")
    total_rows = coefficients.shape[0] * lax.axis_size("ga")
    band_rms = jnp.sqrt(squares / total_rows + 1e-06)
    return ((rotated / band_rms).astype(jnp.bfloat16), band_rms)


def solution(mesh):
    in_specs = (P("ga", "ba"), P("ga", "ba"))
    out_specs = (P("ga", "ba"), P("ba"))
    return jax.shard_map(body, mesh=mesh, in_specs=in_specs, out_specs=out_specs, check_vma=False)
```

profile of v0, /device:TPU:1, one launch (start us, length us, event | category | flops | bytes accessed | tf_op | source)
XLA Modules:
  0.0 259.9 jit_solution(9544626655196929457)
XLA Ops:
  7.2 0.0 all-gather.2.cloned.1.call-start
  7.2 0.7 all-gather.2.cloned.1.call-update
  7.9 6.3 %copy.6 = bf16[1280,1536]{0,1:T(8,128)(2,1)} copy(bf16[1280,1536]{1,0:T(8,128)(2,1)} %param.2) | data formatting | bytes 7864320 | tf_op args[0]
  14.2 3.8 %broadcast_in_dim.7 = bf16[4,1280,1536]{1,2,0:T(8,128)(2,1)S(1)} broadcast(bf16[1280,1536]{0,1:T(8,128)(2,1)} %copy.6), dimensions={1,2} | broadcast | bytes 19660800 | tf_op jit(solution)/shard_map/broadcast_in_dim | solution.py:8
  17.9 176.6 %all_to_all.11 = bf16[4,1280,1536]{1,2,0:T(8,128)(2,1)} all-to-all(bf16[4,1280,1536]{1,2,0:T(8,128)(2,1)S(1)} %broadcast_in_dim.7), channel_id=1, replica_groups=mesh['ga'=32,'ba'=4] {'ba'}, dimensions={0} | all-to-all | bytes 31457280 | tf_op jit(solution)/shard_map/all_to_all | solution.py:9
  194.5 0.0 all-gather.2.cloned.1.call-done
  194.5 34.0 %multiply_reduce_fusion = (f32[1536]{0:T(1024)S(1)}, f32[1280,1536]{1,0:T(8,128)}) fusion(bf16[1280,6144]{0,1:T(8,128)(2,1)} %bitcast.5, bf16[6144,1536]{1,0:T(8,128)(2,1)} %all-gather.2.cloned.1.call-done), kind=kOutput, calls=%fused_computation.1 | convolution fusion | flops 24163121152 | bytes 42473472 | tf_op jit(solution)/shard_map/dot_general | solution.py:30
  228.5 0.1 broadcast_in_dim.8
  228.6 18.1 %all_to_all.12 = f32[32,1,1536]{2,1,0:T(1,128)S(1)} all-to-all(f32[32,1,1536]{2,1,0:T(1,128)S(1)} %broadcast_in_dim.8), channel_id=1, replica_groups=mesh['ga'=32,'ba'=4] {'ga'}, dimensions={0} | all-to-all | bytes 393216 | tf_op jit(solution)/shard_map/all_to_all | solution.py:9
  246.7 0.1 reduce_sum.19
  246.9 0.0 copy-start
  246.9 6.2 %divide_convert_fusion = bf16[1280,1536]{1,0:T(8,128)(2,1)} fusion(f32[1280,1536]{1,0:T(8,128)} %get-tuple-element.3, f32[1536]{0:T(1024)S(1)} %add_sqrt_fusion), kind=kLoop, calls=%fused_computation | loop fusion | flops 3932160 | bytes 11802624 | tf_op jit(solution)/shard_map/convert_element_type | solution.py:36
  253.1 0.0 copy-done
  (1 shorter events, 0.0 us)
Async XLA Ops:
  7.2 187.3 %all-gather.2.cloned.1.call-start = ((), (), s32[]{:S(2)}) async-start(), calls=%async_computation.2 | async-start | bytes 19464192 | tf_op jit(solution)/shard_map/all_gather | solution.py:29
  246.9 6.2 %copy-start = (f32[1536]{0:T(1024)}, f32[1536]{0:T(1024)S(1)}, u32[]{:S(2)}) copy-start(f32[1536]{0:T(1024)S(1)} %add_sqrt_fusion) | copy-start | bytes 18436
Sparse Core Ops, SparseCore 0:
  10.2 81.1 all-gather.1
where the time goes:
time: 260 us
  blocking collectives  195 us (75%)
  matrix products  34 us (13%)
  between operations  14 us (5%)
  local copies, waits for them, and re-layouts  10.1 us (4%)
  other arithmetic  6.32 us (2%)
    all_to_all x2, blocking collectives, copy_for_each(): return lax.all_to_all(copies, axis, split_axis=0, concat_axis=0, tiled=True)  195 us
    dot_general x1, matrix products, body(): jnp.dot(gather_directly(coefficients, 'ba', 1), column_block, preferred_e...  34 us
    unnamed x3, local copies, waits for them, and re-layouts  6.27 us
    convert_element_type x1, other arithmetic, body(): return ((rotated / band_rms).astype(jnp.bfloat16), band_rms)  6.18 us
  transfers between devices with their start and end apart: 1, of which 0 were waited for; matrix products, arithmetic and copies ran while one was open for 4% of the time, Pallas kernels for 0%

commit v1 on v0

v1 whole, which is shorter than its diff:
```python
import functools

import jax
import jax.numpy as jnp
from jax import lax
from jax.experimental import pallas as pl
from jax.experimental.pallas import tpu as pltpu
from jax.sharding import PartitionSpec as P


LAST = 128
OFFSETS = (0, -1, 1, 2)


def plane(shift_of):
    pairs = []
    for z in range(4):
        for y in range(4):
            for c in range(2):
                tz, ty, tc = shift_of(z, y, c)
                pairs.append((z * 8 + y * 2 + c, (tz % 4) * 8 + (ty % 4) * 2 + tc))
    return pairs


def first_axis(step):
    return plane(lambda z, y, c: (z, y + step, c) if c == 0 else (z + step, y, c))


def second_axis(step):
    return plane(lambda z, y, c: (z + step, y, c) if c == 0 else (z, y + step, c))


def gather4(own, ring):
    half = own.shape[0] // 2
    left = lax.ppermute(own, "ga", ring(1))
    right = lax.ppermute(own, "ga", ring(-1))
    far_a = lax.ppermute(left[:half], "ga", ring(1))
    far_b = lax.ppermute(right[half:], "ga", ring(-1))
    return [own, left, right, far_a, far_b]


def piece_offsets(pieces, sub):
    found = []
    for array, offset, base in zip(range(5), (0, -1, 1, 2, 2), (0, 0, 0, 0, 2)):
        for j in range(pieces[array].shape[0] // sub):
            found.append((array, j * sub, offset, OFFSETS[base + j]))
    return found


def first_kernel(layout, sub, *refs):
    n_r = 10
    r_refs, (own, l0, l1, r0, r1) = refs[:n_r], refs[n_r : n_r + 5]
    total, r_far, r_all, a_all, r_sem, a_sem = refs[n_r + 5 :]
    ga, x = lax.axis_index("ga"), lax.axis_index("ba")
    z, y, c = ga // 8, (ga // 2) % 4, ga % 2
    depth = own.shape[1]
    half = l0.shape[0]
    copies = []
    for which in range(2):
        core = c if which == 0 else 1 - c
        for array, row, near, far in layout:
            zz = jnp.where(core == 0, z + near, z + far)
            yy = jnp.where(core == 0, y + far, y + near)
            zz, yy = (zz + 4) % 4, (yy + 4) % 4
            slot = (zz - x + 5) % 4
            at = pl.multiple_of(slot * depth + (yy * 2 + core) * sub, 64)
            copies.append(
                pltpu.make_async_copy(
                    r_refs[which * 5 + array].at[pl.ds(row, sub)],
                    r_all.at[pl.ds(at, sub)],
                    r_sem,
                )
            )
    for ref, row, col in ((l0, 0, 0), (l1, half, 0), (own, 0, depth), (r0, 0, 2 * depth), (r1, half, 2 * depth)):
        copies.append(
            pltpu.make_async_copy(
                ref, a_all.at[pl.ds(row, ref.shape[0]), pl.ds(col, depth)], a_sem
            )
        )
    for copy in copies:
        copy.start()
    for copy in copies:
        copy.wait()
    r_far[...] = r_all[3 * depth :]
    tm, tn = 256, 512
    n_n = total.shape[1] // tn

    def tile(i, carry):
        rows = pl.ds(pl.multiple_of((i // n_n) * tm, tm), tm)
        cols = pl.ds(pl.multiple_of((i % n_n) * tn, tn), tn)
        total[rows, cols] = jnp.dot(
            a_all[rows, :], r_all[: 3 * depth, cols], preferred_element_type=jnp.float32
        )
        return carry

    lax.fori_loop(0, (total.shape[0] // tm) * n_n, tile, 0)


def last_kernel(tops, r_far, before, *refs):
    top, bottom, total_in, total, squares = refs[0], refs[1], refs[3], refs[4], refs[5]
    del r_far, before, total_in
    r = refs[2]
    tm, tn = 128, 512
    n_n = total.shape[1] // tn
    squares[...] = jnp.zeros_like(squares)
    for piece, start in zip((top, bottom), tops):

        def tile(i, carry, piece=piece, start=start):
            cols = pl.ds(pl.multiple_of((i % n_n) * tn, tn), tn)
            row = pl.multiple_of((i // n_n) * tm, tm)
            rows = pl.ds(pl.multiple_of(start + row, tm), tm)
            value = total[rows, cols] + jnp.dot(
                piece[pl.ds(row, tm), :], r[:, cols], preferred_element_type=jnp.float32
            )
            total[rows, cols] = value
            squares[:, cols] += jnp.sum((value * value).reshape(tm // 8, 8, tn), axis=0)
            return carry

        lax.fori_loop(0, (piece.shape[0] // tm) * n_n, tile, 0)


def normalize_kernel(count, total, everyone, new, band_rms, out, sem):
    squares = jnp.sum(everyone[...], axis=0, keepdims=True)
    rms = jnp.sqrt(squares / count + 1e-06)
    band_rms[...] = rms
    inverse = 1.0 / rms
    tm = 128
    steps = total.shape[0] // tm

    def copy(i):
        rows = pl.ds(pl.multiple_of(i * tm, tm), tm)
        return pltpu.make_async_copy(out.at[rows], new.at[rows], sem)

    def tile(i, carry):
        rows = pl.ds(pl.multiple_of(i * tm, tm), tm)
        out[rows, :] = (total[rows, :] * inverse).astype(out.dtype)
        copy(i).start()
        return carry

    lax.fori_loop(0, steps, tile, 0)
    pltpu.make_async_copy(out, new, sem).wait()


def finish(top, bottom, r_far, total, tops):
    rows, columns = total.shape
    vmem = pl.BlockSpec(memory_space=pltpu.VMEM)
    return pl.pallas_call(
        functools.partial(last_kernel, tops, None, None),
        out_shape=(
            jax.ShapeDtypeStruct((rows, columns), jnp.float32),
            jax.ShapeDtypeStruct((8, columns), jnp.float32),
        ),
        in_specs=[vmem] * 4,
        out_specs=(vmem, vmem),
        input_output_aliases={3: 0},
        cost_estimate=pl.CostEstimate(
            flops=2 * 2 * top.shape[0] * r_far.shape[0] * columns,
            bytes_accessed=4 * top.shape[0] * columns,
            transcendentals=0,
        ),
        compiler_params=pltpu.CompilerParams(vmem_limit_bytes=24 * 2**20),
    )(top, bottom, r_far, total)


def program(a, r):
    rows, depth = a.shape
    columns = r.shape[1]
    sub = r.shape[0]
    half = rows // 2
    to_right = [(i, (i + 1) % 4) for i in range(4)]
    to_left = [(i, (i + 3) % 4) for i in range(4)]
    top, bottom = a[:half], a[half:]

    l0 = lax.ppermute(top, "ba", to_right)
    r1 = lax.ppermute(bottom, "ba", to_left)
    l1 = lax.ppermute(bottom, "ba", to_right)
    r0 = lax.ppermute(top, "ba", to_left)
    cut = half - LAST
    far_t0 = lax.ppermute(l0[:cut], "ba", to_right)
    far_b0 = lax.ppermute(r1[:cut], "ba", to_left)
    far_t1 = lax.ppermute(l0[cut:], "ba", to_right)
    far_b1 = lax.ppermute(r1[cut:], "ba", to_left)

    inner = gather4(r, first_axis)
    ring = gather4(jnp.concatenate(inner, axis=0), second_axis)
    swap = plane(lambda z, y, c: (z, y, 1 - c))
    other = [lax.ppermute(piece, "ga", swap) for piece in ring]

    layout = piece_offsets(ring, sub)
    any_space = pl.BlockSpec(memory_space=pl.ANY)
    vmem = pl.BlockSpec(memory_space=pltpu.VMEM)
    total, r_far = pl.pallas_call(
        functools.partial(first_kernel, layout, sub),
        out_shape=(
            jax.ShapeDtypeStruct((rows, columns), jnp.float32),
            jax.ShapeDtypeStruct((depth, columns), jnp.bfloat16),
        ),
        in_specs=[any_space] * 15,
        out_specs=(vmem, vmem),
        scratch_shapes=[
            pltpu.VMEM((4 * depth, columns), jnp.bfloat16),
            pltpu.VMEM((rows, 3 * depth), jnp.bfloat16),
            pltpu.SemaphoreType.DMA,
            pltpu.SemaphoreType.DMA,
        ],
        cost_estimate=pl.CostEstimate(
            flops=2 * rows * 3 * depth * columns,
            bytes_accessed=2 * (rows * 3 * depth + 4 * depth * columns),
            transcendentals=0,
        ),
        compiler_params=pltpu.CompilerParams(vmem_limit_bytes=42 * 2**20),
        name="first",
    )(*ring, *other, a, l0, l1, r0, r1)
    total, squares_a = finish(far_t0, far_b0, r_far, total, (0, half))
    total, squares_b = finish(far_t1, far_b1, r_far, total, (cut, half + cut))
    squares = jnp.sum(squares_a + squares_b, axis=0)
    n = lax.axis_size("ga")
    everyone = lax.all_to_all(
        jnp.broadcast_to(squares, (n, 1, columns)), "ga", split_axis=0, concat_axis=0, tiled=True
    )
    new, band_rms = pl.pallas_call(
        functools.partial(normalize_kernel, rows * n),
        out_shape=(
            jax.ShapeDtypeStruct((rows, columns), jnp.bfloat16),
            jax.ShapeDtypeStruct((1, columns), jnp.float32),
        ),
        in_specs=[vmem, vmem],
        out_specs=(any_space, vmem),
        scratch_shapes=[
            pltpu.VMEM((rows, columns), jnp.bfloat16),
            pltpu.SemaphoreType.DMA,
        ],
        cost_estimate=pl.CostEstimate(
            flops=2 * rows * columns, bytes_accessed=6 * rows * columns, transcendentals=0
        ),
        compiler_params=pltpu.CompilerParams(vmem_limit_bytes=24 * 2**20),
        name="normalize",
    )(total, everyone.reshape(n, columns))
    return new, band_rms.reshape(columns)


def solution(mesh):
    in_specs = (P("ga", "ba"), P("ga", "ba"))
    out_specs = (P("ga", "ba"), P("ba"))
    return jax.shard_map(program, mesh=mesh, in_specs=in_specs, out_specs=out_specs, check_vma=False)
```

time: 260 us -> 193 us (0.74)
  blocking collectives: 195 us -> 15.6 us
  waiting for transfers between devices: 0.68 us -> 92 us
  Pallas kernels: 0 us -> 44.9 us
  matrix products: 34 us -> 0 us
  starting transfers between devices: 0.04 us -> 30.9 us
  between operations: 14 us -> 0.92 us
  other arithmetic: 6.32 us -> 0.64 us
    all_to_all x2 -> x1, blocking collectives: 195 us -> 15.6 us  [program(): lax.all_to_all(jnp.broadcast_to(squares, (n, 1, columns)), 'ga', split_ax...]
    ppermute x0 -> x21, waiting for transfers between devices: none -> 92 us  [the longest x1 39.4 us: program(): l1 = lax.ppermute(bottom, 'ba', to_right)]
    pallas_call x0 -> x4, Pallas kernels: none -> 44.9 us  [the longest x1 31.2 us: program(): pl.pallas_call(functools.partial(first_kernel, layout, sub), out_shape=(j...]
    dot_general x1 -> x0, matrix products: 34 us -> none  [body(): jnp.dot(gather_directly(coefficients, 'ba', 1), column_block, preferred_e...]
    ppermute x0 -> x21, starting transfers between devices: none -> 30.9 us  [the longest x5 7.31 us: program(): other = [lax.ppermute(piece, 'ga', swap) for piece in ring]]
    convert_element_type x1 -> x0, other arithmetic: 6.18 us -> none  [body(): return ((rotated / band_rms).astype(jnp.bfloat16), band_rms)]
    broadcast_in_dim x2 -> x1, local copies, waits for them, and re-layouts: 3.87 us -> 0.1 us  [program(): jnp.broadcast_to(squares, (n, 1, columns))]
    unnamed x3 -> x23, local copies, waits for them, and re-layouts: 6.27 us -> 6.84 us
  transfers between devices with their start and end apart: 1 -> 21, of which waited for: 0 -> 7; matrix products, arithmetic and copies ran while one was open for 4% -> 1% of each run, Pallas kernels for 0% -> 21%
where the time goes in v1:
time: 193 us
  waiting for transfers between devices  92 us (48%)
  Pallas kernels  44.9 us (23%)
  starting transfers between devices  30.9 us (16%)
  blocking collectives  15.6 us (8%)
  local copies, waits for them, and re-layouts  7.68 us (4%)
    ppermute x1, waiting for transfers between devices, program(): l1 = lax.ppermute(bottom, 'ba', to_right)  39.4 us
    pallas_call x1, Pallas kernels, program(): pl.pallas_call(functools.partial(first_kernel, layout, sub), out_shape=(j...  31.2 us
    ppermute x2, waiting for transfers between devices, gather4(): left = lax.ppermute(own, 'ga', ring(1))  29.9 us
    all_to_all x1, blocking collectives, program(): lax.all_to_all(jnp.broadcast_to(squares, (n, 1, columns)), 'ga', split_ax...  15.6 us
    pallas_call x2, Pallas kernels, finish(): pl.pallas_call(functools.partial(last_kernel, tops, None, None), out_shap...  11.6 us
    ppermute x1, waiting for transfers between devices, program(): l0 = lax.ppermute(top, 'ba', to_right)  10.9 us
    ppermute x5, waiting for transfers between devices, program(): other = [lax.ppermute(piece, 'ga', swap) for piece in ring]  7.52 us
    ppermute x5, starting transfers between devices, program(): other = [lax.ppermute(piece, 'ga', swap) for piece in ring]  7.31 us
  transfers between devices with their start and end apart: 21, of which 7 were waited for; matrix products, arithmetic and copies ran while one was open for 1% of the time, Pallas kernels for 21%

profile of v1, /device:TPU:1, one launch (start us, length us, event | category | flops | bytes accessed | tf_op | source)
XLA Modules:
  0.0 192.6 jit_solution(10967700333846601442)
XLA Ops:
  0.6 2.5 %collective-permute-start.4 = (bf16[192,1536]{1,0:T(8,128)(2,1)}, bf16[192,1536]{1,0:T(8,128)(2,1)S(1)}, u32[]{:S(2)}, u32[]{:S(2)}) collective-permute-start(bf16[192,1536]{1,0:T(8,128)(2,1)} %param.3), channel_id=1, source_target_pairs={{0,8},{4,36},{8,16},{12,44},{16,24},{20,52},{24,0},{28,60},{32,40}... | collective-permute-start | bytes 1769480 | tf_op jit(solution)/shard_map/ppermute | solution.py:35
  3.2 2.2 %collective-permute-start.5 = (bf16[192,1536]{1,0:T(8,128)(2,1)}, bf16[192,1536]{1,0:T(8,128)(2,1)S(1)}, u32[]{:S(2)}, u32[]{:S(2)}) collective-permute-start(bf16[192,1536]{1,0:T(8,128)(2,1)} %param.3), channel_id=1, source_target_pairs={{0,24},{4,100},{8,0},{12,108},{16,8},{20,116},{24,16},{28,124},{32... | collective-permute-start | bytes 1769480 | tf_op jit(solution)/shard_map/ppermute | solution.py:36
  5.4 1.1 constant_dynamic-update-slice_fusion.4
  6.5 0.0 copy-start.2
  6.5 6.5 %collective-permute-done.4 = bf16[192,1536]{1,0:T(8,128)(2,1)S(1)} collective-permute-done((bf16[192,1536]{1,0:T(8,128)(2,1)}, bf16[192,1536]{1,0:T(8,128)(2,1)S(1)}, u32[]{:S(2)}, u32[]{:S(2)}) %collective-permute-start.4) | collective-permute-done | bytes 589856 | tf_op jit(solution)/shard_map/ppermute | solution.py:35
  13.0 0.1 collective-permute-start.6
  13.1 0.0 collective-permute-done.5
  13.1 2.8 %collective-permute-start.7 = (bf16[96,1536]{1,0:T(8,128)(2,1)S(1)}, bf16[96,1536]{1,0:T(8,128)(2,1)S(1)}, u32[]{:S(2)}, u32[]{:S(2)}) collective-permute-start(bf16[96,1536]{1,0:T(8,128)(2,1)S(1)} %slice.43), channel_id=1, source_target_pairs={{0,24},{4,100},{8,0},{12,108},{16,8},{20,116},{24,16},{28,124},{32... | collective-permute-start | bytes 884744 | tf_op jit(solution)/shard_map/ppermute | solution.py:38
  16.0 4.2 %collective-permute-done.6 = bf16[96,1536]{1,0:T(8,128)(2,1)S(1)} collective-permute-done((bf16[96,1536]{1,0:T(8,128)(2,1)S(1)}, bf16[96,1536]{1,0:T(8,128)(2,1)S(1)}, u32[]{:S(2)}, u32[]{:S(2)}) %collective-permute-start.6) | collective-permute-done | bytes 294944 | tf_op jit(solution)/shard_map/ppermute | solution.py:37
  20.2 0.0 collective-permute-done.7
  20.2 0.0 copy-start.6
  20.2 0.8 collective-permute-start.8
  21.1 2.1 %collective-permute-start.9 = (bf16[768,1536]{1,0:T(8,128)(2,1)S(1)}, bf16[768,1536]{1,0:T(8,128)(2,1)S(1)}, u32[]{:S(2)}, u32[]{:S(2)}) collective-permute-start(bf16[768,1536]{1,0:T(8,128)(2,1)S(1)} %constant_dynamic-update-slice_fusion.refs_0_), channel_id=1, source_target_pairs={{0,96},{4,28},{8,104},{12,4},{16,112},{20,12},{24,120},{28,20},{32... | collective-permute-start | bytes 7077896 | tf_op jit(solution)/shard_map/ppermute | solution.py:36
  23.2 0.0 copy-done.2
  23.2 0.3 fusion
  23.4 1.3 collective-permute-start
  24.7 1.5 collective-permute-start.2
  26.2 0.0 collective-permute-start.17
  26.2 23.4 %collective-permute-done.8.refs_1_ = bf16[768,1536]{1,0:T(8,128)(2,1)S(1)} collective-permute-done((bf16[768,1536]{1,0:T(8,128)(2,1)S(1)}, bf16[768,1536]{1,0:T(8,128)(2,1)S(1)}, u32[]{:S(2)}, u32[]{:S(2)}) %collective-permute-start.8) | collective-permute-done | bytes 2359328 | tf_op jit(solution)/shard_map/ppermute | solution.py:35
  49.6 2.5 %collective-permute-start.18 = (bf16[640,1536]{1,0:T(8,128)(2,1)S(1)}, bf16[640,1536]{1,0:T(8,128)(2,1)S(1)}, u32[]{:S(2)}, u32[]{:S(2)}) collective-permute-start(bf16[640,1536]{1,0:T(8,128)(2,1)S(1)} %get-tuple-element.19), channel_id=1, source_target_pairs={{0,3},{1,0},{2,1},{3,2},{4,7},{5,4},{6,5},{7,6},{8,11},{9,8},{10,9... | collective-permute-start | bytes 5898248 | tf_op jit(solution)/shard_map/ppermute | solution.py:177
  52.1 0.1 slice.44
  52.2 0.0 collective-permute-done.9.refs_2_
  52.2 0.0 copy-done.6
  52.2 0.0 copy-start.5
  52.2 3.3 %collective-permute-start.12 = (bf16[768,1536]{1,0:T(8,128)(2,1)S(1)}, bf16[768,1536]{1,0:T(8,128)(2,1)S(1)}, u32[]{:S(2)}, u32[]{:S(2)}) collective-permute-start(bf16[768,1536]{1,0:T(8,128)(2,1)S(1)} %constant_dynamic-update-slice_fusion.refs_0_), channel_id=1, source_target_pairs={{0,4},{4,0},{8,12},{12,8},{16,20},{20,16},{24,28},{28,24},{32,36},... | collective-permute-start | bytes 7077896 | tf_op jit(solution)/shard_map/ppermute | solution.py:187
  55.5 0.1 slice.45
  55.6 10.9 %collective-permute-done.refs_11_ = bf16[640,1536]{1,0:T(8,128)(2,1)S(1)} collective-permute-done((bf16[640,1536]{1,0:T(8,128)(2,1)S(1)}, bf16[640,1536]{1,0:T(8,128)(2,1)S(1)}, u32[]{:S(2)}, u32[]{:S(2)}) %collective-permute-start) | collective-permute-done | bytes 1966112 | tf_op jit(solution)/shard_map/ppermute | solution.py:174
  66.5 0.0 collective-permute-start.10
  66.5 0.0 collective-permute-done.2.refs_14_
  66.5 2.7 %collective-permute-start.11 = (bf16[384,1536]{1,0:T(8,128)(2,1)S(1)}, bf16[384,1536]{1,0:T(8,128)(2,1)S(1)}, u32[]{:S(2)}, u32[]{:S(2)}) collective-permute-start(bf16[384,1536]{1,0:T(8,128)(2,1)S(1)} %slice.45), channel_id=1, source_target_pairs={{0,96},{4,28},{8,104},{12,4},{16,112},{20,12},{24,120},{28,20},{32... | collective-permute-start | bytes 3538952 | tf_op jit(solution)/shard_map/ppermute | solution.py:38
  69.2 39.4 %collective-permute-done.17.refs_12_ = bf16[640,1536]{1,0:T(8,128)(2,1)S(1)} collective-permute-done((bf16[640,1536]{1,0:T(8,128)(2,1)S(1)}, bf16[640,1536]{1,0:T(8,128)(2,1)S(1)}, u32[]{:S(2)}, u32[]{:S(2)}) %collective-permute-start.17) | collective-permute-done | bytes 1966112 | tf_op jit(solution)/shard_map/ppermute | solution.py:176
  108.6 3.5 %collective-permute-start.13 = (bf16[768,1536]{1,0:T(8,128)(2,1)S(1)}, bf16[768,1536]{1,0:T(8,128)(2,1)S(1)}, u32[]{:S(2)}, u32[]{:S(2)}) collective-permute-start(bf16[768,1536]{1,0:T(8,128)(2,1)S(1)} %collective-permute-done.8.refs_1_), channel_id=1, source_target_pairs={{0,4},{4,0},{8,12},{12,8},{16,20},{20,16},{24,28},{28,24},{32,36},... | collective-permute-start | bytes 7077896 | tf_op jit(solution)/shard_map/ppermute | solution.py:187
  112.1 0.0 collective-permute-done.18.refs_13_
  112.1 0.1 collective-permute-start.14
  112.2 0.0 collective-permute-done.10.refs_3_
  112.2 0.4 collective-permute-start.15
  112.6 0.0 collective-permute-done.11.refs_4_
  112.6 0.1 collective-permute-start.16
  112.7 0.1 slice.46
  112.8 0.0 copy-done.5
  112.9 0.1 slice.47
  113.0 0.0 collective-permute-done.12.refs_5_
  113.0 1.2 collective-permute-start.19
  114.2 7.1 %collective-permute-done.15.refs_8_ = bf16[384,1536]{1,0:T(8,128)(2,1)S(1)} collective-permute-done((bf16[384,1536]{1,0:T(8,128)(2,1)S(1)}, bf16[384,1536]{1,0:T(8,128)(2,1)S(1)}, u32[]{:S(2)}, u32[]{:S(2)}) %collective-permute-start.15) | collective-permute-done | bytes 1179680 | tf_op jit(solution)/shard_map/ppermute | solution.py:187
  121.3 1.3 collective-permute-start.20
  122.6 0.4 collective-permute-done.16.refs_9_
  123.0 0.0 collective-permute-start.1
  123.0 0.0 collective-permute-done.13.refs_6_
  123.0 2.7 %collective-permute-start.3 = (bf16[128,1536]{1,0:T(8,128)(2,1)S(1)}, bf16[128,1536]{1,0:T(8,128)(2,1)S(1)}, u32[]{:S(2)}, u32[]{:S(2)}) collective-permute-start(bf16[128,1536]{1,0:T(8,128)(2,1)S(1)} %slice.41), channel_id=1, source_target_pairs={{0,3},{1,0},{2,1},{3,2},{4,7},{5,4},{6,5},{7,6},{8,11},{9,8},{10,9... | collective-permute-start | bytes 1179656 | tf_op jit(solution)/shard_map/ppermute | solution.py:182
  125.7 0.0 copy-done.7
  125.7 0.0 collective-permute-done.14.refs_7_
  125.7 31.2 %first.1 = (f32[1280,1536]{1,0:T(8,128)}, bf16[1536,1536]{1,0:T(8,128)(2,1)}) custom-call(bf16[768,1536]{1,0:T(8,128)(2,1)} %copy-done.6, bf16[768,1536]{1,0:T(8,128)(2,1)} %copy-done.4, bf16[768,1536]{1,0:T(8,128)(2,1)} %copy-done.5, bf16[384,1536]{1,0:T(8,128)(2,1)S(1)} %collective-permute-done.10.refs_3_, ...), custom_call_target="tpu_custom_call" | custom-call | flops 18119393280 | bytes 30670848 | tf_op jit(solution)/shard_map/first/pallas_call | solution.py:192
  156.9 0.0 collective-permute-done.19.refs_0_
  156.9 0.0 collective-permute-done.20.refs_1_
  157.0 3.2 %copy-done = f32[1280,1536]{1,0:T(8,128)S(1)} copy-done((f32[1280,1536]{1,0:T(8,128)S(1)}, f32[1280,1536]{1,0:T(8,128)}, u32[]{:S(2)}) %copy-start) | copy-done | bytes 7864344
  160.2 2.3 %copy-done.1 = bf16[1536,1536]{1,0:T(8,128)(2,1)S(1)} copy-done((bf16[1536,1536]{1,0:T(8,128)(2,1)S(1)}, bf16[1536,1536]{1,0:T(8,128)(2,1)}, u32[]{:S(2)}) %copy-start.1) | copy-done | bytes 4718616
  162.5 9.3 %shard_map.41 = (f32[1280,1536]{1,0:T(8,128)S(1)}, f32[8,1536]{1,0:T(8,128)S(1)}) custom-call(bf16[512,1536]{1,0:T(8,128)(2,1)S(1)} %collective-permute-done.19.refs_0_, bf16[512,1536]{1,0:T(8,128)(2,1)S(1)} %collective-permute-done.20.refs_1_, bf16[1536,1536]{1,0:T(8,128)(2,1)S(1)} %copy-done.1, ...), custom_call_target="tpu_custom_call", output_to_operand_aliasing={{0}: (3, {})} | custom-call | flops 4831838208 | bytes 3145728 | tf_op jit(solution)/shard_map/pallas_call | solution.py:147
  171.8 0.0 collective-permute-done.1.refs_0_
  171.8 0.0 collective-permute-done.3.refs_1_
  171.8 2.3 %shard_map.42 = (f32[1280,1536]{1,0:T(8,128)S(1)}, f32[8,1536]{1,0:T(8,128)S(1)}) custom-call(bf16[128,1536]{1,0:T(8,128)(2,1)S(1)} %collective-permute-done.1.refs_0_, bf16[128,1536]{1,0:T(8,128)(2,1)S(1)} %collective-permute-done.3.refs_1_, bf16[1536,1536]{1,0:T(8,128)(2,1)S(1)} %copy-done.1, ...), custom_call_target="tpu_custom_call", output_to_operand_aliasing={{0}: (3, {})} | custom-call | flops 1207959552 | bytes 786432 | tf_op jit(solution)/shard_map/pallas_call | solution.py:147
  174.2 0.1 broadcast_in_dim.3
  174.3 15.6 %all_to_all.5 = f32[32,1,1536]{2,1,0:T(1,128)S(1)} all-to-all(f32[32,1,1536]{2,1,0:T(1,128)S(1)} %broadcast_in_dim.3), channel_id=1, replica_groups=mesh['ga'=32,'ba'=4] {'ga'}, dimensions={0} | all-to-all | bytes 393216 | tf_op jit(solution)/shard_map/all_to_all | solution.py:218
  189.9 2.0 %normalize.1 = (bf16[1280,1536]{1,0:T(8,128)(2,1)}, f32[1,1536]{1,0:T(1,128)S(1)}) custom-call(f32[1280,1536]{1,0:T(8,128)S(1)} %get-tuple-element.13.total, f32[32,1536]{1,0:T(8,128)S(1)} %bitcast.3), custom_call_target="tpu_custom_call" | custom-call | flops 3932160 | bytes 11796480 | tf_op jit(solution)/shard_map/normalize/pallas_call | solution.py:221
  191.9 0.6 reduce
  (19 shorter events, 0.3 us)
Async XLA Ops:
  0.6 12.4 %collective-permute-start.4 = (bf16[192,1536]{1,0:T(8,128)(2,1)}, bf16[192,1536]{1,0:T(8,128)(2,1)S(1)}, u32[]{:S(2)}, u32[]{:S(2)}) collective-permute-start(bf16[192,1536]{1,0:T(8,128)(2,1)} %param.3), channel_id=1, source_target_pairs={{0,8},{4,36},{8,16},{12,44},{16,24},{20,52},{24,0},{28,60},{32,40}... | collective-permute-start | bytes 1769480 | tf_op jit(solution)/shard_map/ppermute | solution.py:35
  3.2 9.9 %collective-permute-start.5 = (bf16[192,1536]{1,0:T(8,128)(2,1)}, bf16[192,1536]{1,0:T(8,128)(2,1)S(1)}, u32[]{:S(2)}, u32[]{:S(2)}) collective-permute-start(bf16[192,1536]{1,0:T(8,128)(2,1)} %param.3), channel_id=1, source_target_pairs={{0,24},{4,100},{8,0},{12,108},{16,8},{20,116},{24,16},{28,124},{32... | collective-permute-start | bytes 1769480 | tf_op jit(solution)/shard_map/ppermute | solution.py:36
  6.5 16.7 %copy-start.2 = (bf16[1280,1536]{1,0:T(8,128)(2,1)S(1)}, bf16[1280,1536]{1,0:T(8,128)(2,1)}, u32[]{:S(2)}) copy-start(bf16[1280,1536]{1,0:T(8,128)(2,1)} %refs_10_.1) | copy-start | bytes 11796484
  13.0 7.1 %collective-permute-start.6 = (bf16[96,1536]{1,0:T(8,128)(2,1)S(1)}, bf16[96,1536]{1,0:T(8,128)(2,1)S(1)}, u32[]{:S(2)}, u32[]{:S(2)}) collective-permute-start(bf16[96,1536]{1,0:T(8,128)(2,1)S(1)} %slice.42), channel_id=1, source_target_pairs={{0,8},{4,36},{8,16},{12,44},{16,24},{20,52},{24,0},{28,60},{32,40}... | collective-permute-start | bytes 884744 | tf_op jit(solution)/shard_map/ppermute | solution.py:37
  13.1 7.1 %collective-permute-start.7 = (bf16[96,1536]{1,0:T(8,128)(2,1)S(1)}, bf16[96,1536]{1,0:T(8,128)(2,1)S(1)}, u32[]{:S(2)}, u32[]{:S(2)}) collective-permute-start(bf16[96,1536]{1,0:T(8,128)(2,1)S(1)} %slice.43), channel_id=1, source_target_pairs={{0,24},{4,100},{8,0},{12,108},{16,8},{20,116},{24,16},{28,124},{32... | collective-permute-start | bytes 884744 | tf_op jit(solution)/shard_map/ppermute | solution.py:38
  20.2 32.0 %copy-start.6 = (bf16[768,1536]{1,0:T(8,128)(2,1)}, bf16[768,1536]{1,0:T(8,128)(2,1)S(1)}, u32[]{:S(2)}) copy-start(bf16[768,1536]{1,0:T(8,128)(2,1)S(1)} %constant_dynamic-update-slice_fusion.refs_0_) | copy-start | bytes 7077892
  20.2 29.4 %collective-permute-start.8 = (bf16[768,1536]{1,0:T(8,128)(2,1)S(1)}, bf16[768,1536]{1,0:T(8,128)(2,1)S(1)}, u32[]{:S(2)}, u32[]{:S(2)}) collective-permute-start(bf16[768,1536]{1,0:T(8,128)(2,1)S(1)} %constant_dynamic-update-slice_fusion.refs_0_), channel_id=1, source_target_pairs={{0,32},{4,12},{8,40},{12,20},{16,48},{20,28},{24,56},{28,4},{32,64... | collective-permute-start | bytes 7077896 | tf_op jit(solution)/shard_map/ppermute | solution.py:35
  21.1 31.1 %collective-permute-start.9 = (bf16[768,1536]{1,0:T(8,128)(2,1)S(1)}, bf16[768,1536]{1,0:T(8,128)(2,1)S(1)}, u32[]{:S(2)}, u32[]{:S(2)}) collective-permute-start(bf16[768,1536]{1,0:T(8,128)(2,1)S(1)} %constant_dynamic-update-slice_fusion.refs_0_), channel_id=1, source_target_pairs={{0,96},{4,28},{8,104},{12,4},{16,112},{20,12},{24,120},{28,20},{32... | collective-permute-start | bytes 7077896 | tf_op jit(solution)/shard_map/ppermute | solution.py:36
  23.4 43.1 %collective-permute-start = (bf16[640,1536]{1,0:T(8,128)(2,1)S(1)}, bf16[640,1536]{1,0:T(8,128)(2,1)S(1)}, u32[]{:S(2)}, u32[]{:S(2)}) collective-permute-start(bf16[640,1536]{1,0:T(8,128)(2,1)S(1)} %get-tuple-element.19), channel_id=1, source_target_pairs={{0,1},{1,2},{2,3},{3,0},{4,5},{5,6},{6,7},{7,4},{8,9},{9,10},{10,1... | collective-permute-start | bytes 5898248 | tf_op jit(solution)/shard_map/ppermute | solution.py:174
  24.7 41.8 %collective-permute-start.2 = (bf16[640,1536]{1,0:T(8,128)(2,1)S(1)}, bf16[640,1536]{1,0:T(8,128)(2,1)S(1)}, u32[]{:S(2)}, u32[]{:S(2)}) collective-permute-start(bf16[640,1536]{1,0:T(8,128)(2,1)S(1)} %get-tuple-element.18), channel_id=1, source_target_pairs={{0,3},{1,0},{2,1},{3,2},{4,7},{5,4},{6,5},{7,6},{8,11},{9,8},{10,9... | collective-permute-start | bytes 5898248 | tf_op jit(solution)/shard_map/ppermute | solution.py:175
  26.2 82.4 %collective-permute-start.17 = (bf16[640,1536]{1,0:T(8,128)(2,1)S(1)}, bf16[640,1536]{1,0:T(8,128)(2,1)S(1)}, u32[]{:S(2)}, u32[]{:S(2)}) collective-permute-start(bf16[640,1536]{1,0:T(8,128)(2,1)S(1)} %get-tuple-element.18), channel_id=1, source_target_pairs={{0,1},{1,2},{2,3},{3,0},{4,5},{5,6},{6,7},{7,4},{8,9},{9,10},{10,1... | collective-permute-start | bytes 5898248 | tf_op jit(solution)/shard_map/ppermute | solution.py:176
  49.6 59.0 %copy-start.4 = (bf16[768,1536]{1,0:T(8,128)(2,1)}, bf16[768,1536]{1,0:T(8,128)(2,1)S(1)}, u32[]{:S(2)}) copy-start(bf16[768,1536]{1,0:T(8,128)(2,1)S(1)} %collective-permute-done.8.refs_1_) | copy-start | bytes 7077892
  49.6 62.5 %collective-permute-start.18 = (bf16[640,1536]{1,0:T(8,128)(2,1)S(1)}, bf16[640,1536]{1,0:T(8,128)(2,1)S(1)}, u32[]{:S(2)}, u32[]{:S(2)}) collective-permute-start(bf16[640,1536]{1,0:T(8,128)(2,1)S(1)} %get-tuple-element.19), channel_id=1, source_target_pairs={{0,3},{1,0},{2,1},{3,2},{4,7},{5,4},{6,5},{7,6},{8,11},{9,8},{10,9... | collective-permute-start | bytes 5898248 | tf_op jit(solution)/shard_map/ppermute | solution.py:177
  52.2 60.6 %copy-start.5 = (bf16[768,1536]{1,0:T(8,128)(2,1)}, bf16[768,1536]{1,0:T(8,128)(2,1)S(1)}, u32[]{:S(2)}) copy-start(bf16[768,1536]{1,0:T(8,128)(2,1)S(1)} %collective-permute-done.9.refs_2_) | copy-start | bytes 7077892
  52.2 60.8 %collective-permute-start.12 = (bf16[768,1536]{1,0:T(8,128)(2,1)S(1)}, bf16[768,1536]{1,0:T(8,128)(2,1)S(1)}, u32[]{:S(2)}, u32[]{:S(2)}) collective-permute-start(bf16[768,1536]{1,0:T(8,128)(2,1)S(1)} %constant_dynamic-update-slice_fusion.refs_0_), channel_id=1, source_target_pairs={{0,4},{4,0},{8,12},{12,8},{16,20},{20,16},{24,28},{28,24},{32,36},... | collective-permute-start | bytes 7077896 | tf_op jit(solution)/shard_map/ppermute | solution.py:187
  66.5 45.7 %collective-permute-start.10 = (bf16[384,1536]{1,0:T(8,128)(2,1)S(1)}, bf16[384,1536]{1,0:T(8,128)(2,1)S(1)}, u32[]{:S(2)}, u32[]{:S(2)}) collective-permute-start(bf16[384,1536]{1,0:T(8,128)(2,1)S(1)} %slice.44), channel_id=1, source_target_pairs={{0,32},{4,12},{8,40},{12,20},{16,48},{20,28},{24,56},{28,4},{32,64... | collective-permute-start | bytes 3538952 | tf_op jit(solution)/shard_map/ppermute | solution.py:37
  66.5 46.5 %copy-start.3 = (bf16[640,1536]{1,0:T(8,128)(2,1)}, bf16[640,1536]{1,0:T(8,128)(2,1)S(1)}, u32[]{:S(2)}) copy-start(bf16[640,1536]{1,0:T(8,128)(2,1)S(1)} %collective-permute-done.2.refs_14_) | copy-start | bytes 5898244
  66.5 46.1 %collective-permute-start.11 = (bf16[384,1536]{1,0:T(8,128)(2,1)S(1)}, bf16[384,1536]{1,0:T(8,128)(2,1)S(1)}, u32[]{:S(2)}, u32[]{:S(2)}) collective-permute-start(bf16[384,1536]{1,0:T(8,128)(2,1)S(1)} %slice.45), channel_id=1, source_target_pairs={{0,96},{4,28},{8,104},{12,4},{16,112},{20,12},{24,120},{28,20},{32... | collective-permute-start | bytes 3538952 | tf_op jit(solution)/shard_map/ppermute | solution.py:38
  108.6 14.4 %collective-permute-start.13 = (bf16[768,1536]{1,0:T(8,128)(2,1)S(1)}, bf16[768,1536]{1,0:T(8,128)(2,1)S(1)}, u32[]{:S(2)}, u32[]{:S(2)}) collective-permute-start(bf16[768,1536]{1,0:T(8,128)(2,1)S(1)} %collective-permute-done.8.refs_1_), channel_id=1, source_target_pairs={{0,4},{4,0},{8,12},{12,8},{16,20},{20,16},{24,28},{28,24},{32,36},... | collective-permute-start | bytes 7077896 | tf_op jit(solution)/shard_map/ppermute | solution.py:187
  112.1 13.6 %collective-permute-start.14 = (bf16[768,1536]{1,0:T(8,128)(2,1)S(1)}, bf16[768,1536]{1,0:T(8,128)(2,1)}, u32[]{:S(2)}, u32[]{:S(2)}) collective-permute-start(bf16[768,1536]{1,0:T(8,128)(2,1)S(1)} %collective-permute-done.9.refs_2_), channel_id=1, source_target_pairs={{0,4},{4,0},{8,12},{12,8},{16,20},{20,16},{24,28},{28,24},{32,36},... | collective-permute-start | bytes 7077896 | tf_op jit(solution)/shard_map/ppermute | solution.py:187
  112.2 9.1 %collective-permute-start.15 = (bf16[384,1536]{1,0:T(8,128)(2,1)S(1)}, bf16[384,1536]{1,0:T(8,128)(2,1)S(1)}, u32[]{:S(2)}, u32[]{:S(2)}) collective-permute-start(bf16[384,1536]{1,0:T(8,128)(2,1)S(1)} %collective-permute-done.10.refs_3_), channel_id=1, source_target_pairs={{0,4},{4,0},{8,12},{12,8},{16,20},{20,16},{24,28},{28,24},{32,36},... | collective-permute-start | bytes 3538952 | tf_op jit(solution)/shard_map/ppermute | solution.py:187
  112.6 10.4 %collective-permute-start.16 = (bf16[384,1536]{1,0:T(8,128)(2,1)S(1)}, bf16[384,1536]{1,0:T(8,128)(2,1)S(1)}, u32[]{:S(2)}, u32[]{:S(2)}) collective-permute-start(bf16[384,1536]{1,0:T(8,128)(2,1)S(1)} %collective-permute-done.11.refs_4_), channel_id=1, source_target_pairs={{0,4},{4,0},{8,12},{12,8},{16,20},{20,16},{24,28},{28,24},{32,36},... | collective-permute-start | bytes 3538952 | tf_op jit(solution)/shard_map/ppermute | solution.py:187
  113.0 12.7 %copy-start.7 = (bf16[768,1536]{1,0:T(8,128)(2,1)}, bf16[768,1536]{1,0:T(8,128)(2,1)S(1)}, u32[]{:S(2)}) copy-start(bf16[768,1536]{1,0:T(8,128)(2,1)S(1)} %collective-permute-done.12.refs_5_) | copy-start | bytes 7077892
  113.0 43.9 %collective-permute-start.19 = (bf16[512,1536]{1,0:T(8,128)(2,1)S(1)}, bf16[512,1536]{1,0:T(8,128)(2,1)S(1)}, u32[]{:S(2)}, u32[]{:S(2)}) collective-permute-start(bf16[512,1536]{1,0:T(8,128)(2,1)S(1)} %slice.46), channel_id=1, source_target_pairs={{0,1},{1,2},{2,3},{3,0},{4,5},{5,6},{6,7},{7,4},{8,9},{9,10},{10,1... | collective-permute-start | bytes 4718600 | tf_op jit(solution)/shard_map/ppermute | solution.py:179
  121.3 35.6 %collective-permute-start.20 = (bf16[512,1536]{1,0:T(8,128)(2,1)S(1)}, bf16[512,1536]{1,0:T(8,128)(2,1)S(1)}, u32[]{:S(2)}, u32[]{:S(2)}) collective-permute-start(bf16[512,1536]{1,0:T(8,128)(2,1)S(1)} %slice.47), channel_id=1, source_target_pairs={{0,3},{1,0},{2,1},{3,2},{4,7},{5,4},{6,5},{7,6},{8,11},{9,8},{10,9... | collective-permute-start | bytes 4718600 | tf_op jit(solution)/shard_map/ppermute | solution.py:180
  123.0 48.8 %collective-permute-start.1 = (bf16[128,1536]{1,0:T(8,128)(2,1)S(1)}, bf16[128,1536]{1,0:T(8,128)(2,1)S(1)}, u32[]{:S(2)}, u32[]{:S(2)}) collective-permute-start(bf16[128,1536]{1,0:T(8,128)(2,1)S(1)} %slice.40), channel_id=1, source_target_pairs={{0,1},{1,2},{2,3},{3,0},{4,5},{5,6},{6,7},{7,4},{8,9},{9,10},{10,1... | collective-permute-start | bytes 1179656 | tf_op jit(solution)/shard_map/ppermute | solution.py:181
  123.0 2.7 %copy-start.8 = (bf16[768,1536]{1,0:T(8,128)(2,1)}, bf16[768,1536]{1,0:T(8,128)(2,1)S(1)}, u32[]{:S(2)}) copy-start(bf16[768,1536]{1,0:T(8,128)(2,1)S(1)} %collective-permute-done.13.refs_6_) | copy-start | bytes 7077892
  123.0 48.8 %collective-permute-start.3 = (bf16[128,1536]{1,0:T(8,128)(2,1)S(1)}, bf16[128,1536]{1,0:T(8,128)(2,1)S(1)}, u32[]{:S(2)}, u32[]{:S(2)}) collective-permute-start(bf16[128,1536]{1,0:T(8,128)(2,1)S(1)} %slice.41), channel_id=1, source_target_pairs={{0,3},{1,0},{2,1},{3,2},{4,7},{5,4},{6,5},{7,6},{8,11},{9,8},{10,9... | collective-permute-start | bytes 1179656 | tf_op jit(solution)/shard_map/ppermute | solution.py:182
  157.0 3.2 %copy-start = (f32[1280,1536]{1,0:T(8,128)S(1)}, f32[1280,1536]{1,0:T(8,128)}, u32[]{:S(2)}) copy-start(f32[1280,1536]{1,0:T(8,128)} %get-tuple-element.11.refs_3_) | copy-start | bytes 23592964
  160.2 2.3 %copy-start.1 = (bf16[1536,1536]{1,0:T(8,128)(2,1)S(1)}, bf16[1536,1536]{1,0:T(8,128)(2,1)}, u32[]{:S(2)}) copy-start(bf16[1536,1536]{1,0:T(8,128)(2,1)} %get-tuple-element.10.refs_2_) | copy-start | bytes 14155780
